TPU v7x, 32 devices: a whole 2x2x4 slice. The times are simulated.
32 devices in a mesh: tile: 8 (over z, x), cls: 4 (over y, core).
Axes of the slice: x: 2, y: 2, z: 4, core: 2. Of those that a mesh axis runs over, the one named last changes fastest.
Arguments:
- concentration: float32 [64, 4, 16384], P('cls', None, 'tile'), may hold values from 0.05 to 2
- velocity: float32 [2, 4, 16384], P(None, None, 'tile'), may hold values from -0.3 to 0.3
- land_mask: int32 [16384], P('tile'), may hold values 0 or 1
- settling: float32 [64], P('cls'), may hold values from 0.01 to 0.3
- breakage_rate: float32 [64], replicated, may hold values from 0.02 to 0.3
- kernel_levels: int32 [64, 64], replicated, may hold values from 100 to 1000, as said below
- pair_target: int32 [64, 64], replicated, may hold values from 0 to 63, as said below
- fragment_weights: int32 [64, 64], replicated, may hold values from 1 to 16
Outputs:
- flocs: float32 [64, 4, 16384], P('cls', None, 'tile')
Inputs may be any that keep to these rules, and one draw needn't show every extreme that they name: `kernel_levels`: symmetric. `pair_target`: symmetric, and entry [i, j] is at least the larger of i and j.
All inputs are finite; a program needn't handle non-finite values. No bound on the sum of `land_mask` on one device may be relied on, other than what follows from the above.
Results may differ from a plain program's by a relative error of at most 0.0001.
Values sent between devices are 32-bit elements; how exact they have to be, the bound alone decides.
A program may use at most 64 MiB of HBM per device.

v0:
```python
import jax
import jax.numpy as jnp
from jax import lax
from jax.sharding import PartitionSpec as P

CY = 512
CX = 4
kernel_scale = 1e-05
temp_floats = 2097152


def passed_along(x, axis, by):
    length = lax.axis_size(axis)
    pairs = [(i, i + by) for i in range(length) if 0 <= i + by < length]
    return lax.ppermute(x, axis, pairs)


def face_flux(low, high, group, part):
    speed = 0.5 * (low[group + part] + high[group + part]) * low[group + 2] * high[group + 2]
    return jnp.maximum(speed, 0.0) * low[:group] + jnp.minimum(speed, 0.0) * high[:group]


def make_tables(start, count, kernel_levels, pair_target, fragment_weights, breakage_rate):
    total = kernel_levels.shape[0]
    levels = kernel_levels.astype(jnp.float32) * kernel_scale
    rank = jnp.arange(total, dtype=jnp.int32)
    mine = start + jnp.arange(count, dtype=jnp.int32)
    hit = pair_target[None, :, :] == mine[:, None, None]
    birth = jnp.where(hit, 0.5 * levels[None, :, :], 0.0)
    pairs = jnp.transpose(birth, (1, 0, 2)).reshape(total * count, total)
    lower = jnp.where(rank[:, None] <= rank[None, :], fragment_weights.astype(jnp.float32), 0.0)
    frag = lower / jnp.sum(lower, axis=0, keepdims=True)
    kernel_rows = lax.dynamic_slice_in_dim(levels, start, count, 0)
    frag_rows = lax.dynamic_slice_in_dim(frag, start, count, 0)
    rate_rows = lax.dynamic_slice_in_dim(breakage_rate, start, count, 0)
    return (pairs, kernel_rows, frag_rows, rate_rows)


def react(own, whole, tables, breakage_rate):
    pairs, kernel_rows, frag_rows, rate_rows = tables
    count, width = own.shape
    total = whole.shape[0]
    block = max(1, min(width, temp_floats // (total * count)))
    while width % block != 0:
        block = block - 1
    steps_count = width // block

    def add_block(index, gain):
        offset = index * block
        cols = lax.dynamic_slice_in_dim(whole, offset, block, 1)
        made = jnp.dot(
            pairs, cols, precision=lax.Precision.HIGHEST, preferred_element_type=jnp.float32
        )
        part_gain = jnp.sum(made.reshape(total, count, block) * cols[:, None, :], axis=0)
        return lax.dynamic_update_slice_in_dim(gain, part_gain, offset, 1)

    gain = lax.fori_loop(0, steps_count, add_block, jnp.zeros((count, width), jnp.float32))
    loss = own * jnp.dot(
        kernel_rows, whole, precision=lax.Precision.HIGHEST, preferred_element_type=jnp.float32
    )
    broken = (
        jnp.dot(
            frag_rows,
            breakage_rate[:, None] * whole,
            precision=lax.Precision.HIGHEST,
            preferred_element_type=jnp.float32,
        )
        - rate_rows[:, None] * own
    )
    return own + gain - loss + broken


def body(
    concentration,
    velocity,
    land_mask,
    settling,
    breakage_rate,
    kernel_levels,
    pair_target,
    fragment_weights,
):
    group, layers, columns = concentration.shape
    field = concentration.reshape(group, layers, CX, CY)
    water = land_mask.astype(jnp.float32).reshape(1, 1, CX, CY)
    stacked = jnp.concatenate(
        [field, velocity.reshape(2, layers, CX, CY), jnp.broadcast_to(water, (1, layers, CX, CY))],
        0,
    )
    west = passed_along(stacked[:, :, CX - 1 :, :], "tile", 1)
    east = passed_along(stacked[:, :, :1, :], "tile", -1)
    along_x = jnp.concatenate([west, stacked, east], 2)
    along_y = jnp.pad(stacked, ((0, 0), (0, 0), (0, 0), (1, 1)))
    flux_x = face_flux(along_x[:, :, :-1], along_x[:, :, 1:], group, 0)
    flux_y = face_flux(along_y[:, :, :, :-1], along_y[:, :, :, 1:], group, 1)
    moved = (
        field
        - (flux_x[:, :, 1:] - flux_x[:, :, :-1])
        - (flux_y[:, :, :, 1:] - flux_y[:, :, :, :-1])
    )
    sink = settling[:, None, None, None] * field
    moved = moved - sink + jnp.pad(sink[:, :-1], ((0, 0), (1, 0), (0, 0), (0, 0)))
    current = moved.reshape(group, layers * columns)
    start = lax.axis_index("cls") * group
    tables = make_tables(start, group, kernel_levels, pair_target, fragment_weights, breakage_rate)
    for sub in range(2):
        whole = lax.all_gather(current, "cls", axis=0, tiled=True)
        current = react(current, whole, tables, breakage_rate)
    return current.reshape(group, layers, columns)


def solution(mesh):
    return jax.shard_map(
        body,
        mesh=mesh,
        in_specs=(
            P("cls", None, "tile"),
            P(None, None, "tile"),
            P("tile"),
            P("cls"),
            P(),
            P(),
            P(),
            P(),
        ),
        out_specs=P("cls", None, "tile"),
        check_vma=False,
    )
```

profile of v0, /device:TPU:0, one launch (start us, length us, event | category | flops | bytes accessed | tf_op | source)
XLA Modules:
  0.0 164.2 jit_solution(15692153921223102179)
XLA Ops:
  6.5 1.5 reshape.47
  10.1 4.9 %collective-permute-start = (f32[19,4,1,512]{3,2,1,0:T(1,128)S(1)}, f32[19,4,1,512]{3,2,1,0:T(1,128)S(1)}, u32[]{:S(2)}, u32[]{:S(2)}) collective-permute-start(f32[19,4,1,512]{3,2,1,0:T(1,128)S(1)} %get-tuple-element.227), channel_id=1, source_target_pairs={{0,4},{4,8},{8,12},{12,16},{16,20},{20,24},{24,28},{1,5},{5,9},{9,... | collective-permute-start | bytes 466952 | tf_op jit(solution)/shard_map/ppermute | solution.py:15
  15.0 1.3 collective-permute-start.1
  17.1 1.2 collective-permute-done
  18.3 4.1 %collective-permute-done.1 = f32[19,4,1,512]{3,2,1,0:T(1,128)S(1)} collective-permute-done((f32[19,4,1,512]{3,2,1,0:T(1,128)S(1)}, f32[19,4,1,512]{3,2,1,0:T(1,128)S(1)}, u32[]{:S(2)}, u32[]{:S(2)}) %collective-permute-start.1) | collective-permute-done | bytes 155680 | tf_op jit(solution)/shard_map/ppermute | solution.py:15
  23.6 1.2 reshape.49
  25.2 23.7 %all-gather.3.cloned.1.call-done = f32[64,8192]{1,0:T(8,128)} async-done(((f32[16,8192]{1,0:T(8,128)}), f32[64,8192]{1,0:T(8,128)}) %all-gather.3.cloned.1.call-update) | async-done | bytes 2097168 | tf_op jit(solution)/shard_map/all_gather | solution.py:107
  49.0 37.6 %while.28 = (s32[]{:T(128)}, f32[16,8192]{1,0:T(8,128)S(1)}, f32[64,8192]{1,0:T(8,128)}, s32[64,64]{1,0:T(8,128)S(1)}, s32[1024]{0:T(1024)S(1)}, /*index=5*/f32[...) while((s32[]{:T(128)}, f32[16,8192]{1,0:T(8,128)S(1)}, f32[64,8192]{1,0:T(8,128)}, ...), condition=%wide.region_2.3_spmd.clone, body=%wide.region_0.2_spmd.clone.sunk | while | flops 1614905344 | bytes 19828892 | solution.py:57
  49.0 1.1 constant_dynamic-slice_fusion.4
  50.3 6.7 %fusion.53 = f32[2048,1024]{0,1:T(8,128)S(1)} fusion(f32[64,2048]{1,0:T(8,128)S(1)} %constant_dynamic-slice_fusion.4, f32[1024,64]{1,0:T(8,128)S(1)} %bitcast_select_fusion.4), kind=kOutput, calls=%fused_computation.77.clone.1 | convolution fusion | flops 1610612736 | bytes 9175040 | tf_op jit(solution)/shard_map/while/body/eval_jaxpr/dot_general | solution.py:51
  57.0 1.4 multiply_reduce_fusion.4
  59.7 6.7 %fusion.53 = f32[2048,1024]{0,1:T(8,128)S(1)} fusion(f32[64,2048]{1,0:T(8,128)S(1)} %constant_dynamic-slice_fusion.4, f32[1024,64]{1,0:T(8,128)S(1)} %bitcast_select_fusion.4), kind=kOutput, calls=%fused_computation.77.clone.1 | convolution fusion | flops 1610612736 | bytes 9175040 | tf_op jit(solution)/shard_map/while/body/eval_jaxpr/dot_general | solution.py:51
  66.4 1.4 multiply_reduce_fusion.4
  69.1 6.7 %fusion.53 = f32[2048,1024]{0,1:T(8,128)S(1)} fusion(f32[64,2048]{1,0:T(8,128)S(1)} %constant_dynamic-slice_fusion.4, f32[1024,64]{1,0:T(8,128)S(1)} %bitcast_select_fusion.4), kind=kOutput, calls=%fused_computation.77.clone.1 | convolution fusion | flops 1610612736 | bytes 9175040 | tf_op jit(solution)/shard_map/while/body/eval_jaxpr/dot_general | solution.py:51
  75.8 1.4 multiply_reduce_fusion.4
  78.5 6.7 %fusion.53 = f32[2048,1024]{0,1:T(8,128)S(1)} fusion(f32[64,2048]{1,0:T(8,128)S(1)} %constant_dynamic-slice_fusion.4, f32[1024,64]{1,0:T(8,128)S(1)} %bitcast_select_fusion.4), kind=kOutput, calls=%fused_computation.77.clone.1 | convolution fusion | flops 1610612736 | bytes 9175040 | tf_op jit(solution)/shard_map/while/body/eval_jaxpr/dot_general | solution.py:51
  85.2 1.4 multiply_reduce_fusion.4
  86.6 2.8 %fusion.7 = f32[16,8192]{1,0:T(8,128)S(1)} fusion(f32[16,8192]{1,0:T(8,128)S(1)} %copy-done.3, f32[64,8192]{1,0:T(8,128)} %get-tuple-element.368, f32[16,8192]{1,0:T(8,128)S(1)} %get-tuple-element.163, f32[64,64]{1,0:T(8,128)S(1)} %convert_element_type.14, s32[]{:T(128)S(6)} %select_n.32), kind=kOutput, calls=%fused_computation.19 | convolution fusion | flops 101057536 | bytes 3678212 | tf_op jit(solution)/shard_map/dot_general | solution.py:58
  89.5 2.0 %fusion.6 = f32[16,8192]{1,0:T(8,128)} fusion(f32[16,8192]{1,0:T(8,128)S(1)} %fusion.7, f32[64,8192]{1,0:T(8,128)S(1)} %copy-done, f32[64]{0:T(128)S(1)} %copy-done.7, f32[16,8192]{1,0:T(8,128)S(1)} %copy-done.3, f32[16]{0:T(128)S(1)} %dynamic_slice.25, f32[64,64]{1,0:T(8,128)S(1)} %get-tuple-element.230, s32[]{:T(128)S(6)} %select_n.32, ...), kind=kOutput, calls=%fused_computation.17 | convolution fusion | flops 101581824 | bytes 3679748 | tf_op jit(solution)/shard_map/dot_general | solution.py:62
  91.5 22.7 %all-gather.5.cloned.1.call-done = f32[64,8192]{1,0:T(8,128)} async-done(((f32[16,8192]{1,0:T(8,128)}), f32[64,8192]{1,0:T(8,128)}) %all-gather.5.cloned.1.call-update) | async-done | bytes 2097168 | tf_op jit(solution)/shard_map/all_gather | solution.py:107
  114.3 37.8 %while.29 = (s32[]{:T(128)}, f32[16,8192]{1,0:T(8,128)S(1)}, f32[64,8192]{1,0:T(8,128)}, s32[64,64]{1,0:T(8,128)S(1)}, s32[1024]{0:T(1024)S(1)}, /*index=5*/f32[...) while((s32[]{:T(128)}, f32[16,8192]{1,0:T(8,128)S(1)}, f32[64,8192]{1,0:T(8,128)}, ...), condition=%wide.region_6.7_spmd.clone, body=%wide.region_4.6_spmd.clone.sunk | while | flops 1614905344 | bytes 19828892 | solution.py:57
  115.8 6.7 %fusion.56 = f32[2048,1024]{0,1:T(8,128)S(1)} fusion(f32[64,2048]{1,0:T(8,128)S(1)} %constant_dynamic-slice_fusion.5, f32[1024,64]{1,0:T(8,128)S(1)} %bitcast_select_fusion.5), kind=kOutput, calls=%fused_computation.78.clone.1 | convolution fusion | flops 1610612736 | bytes 9175040 | tf_op jit(solution)/shard_map/while/body/eval_jaxpr/dot_general | solution.py:51
  122.5 1.4 multiply_reduce_fusion.5
  125.2 6.7 %fusion.56 = f32[2048,1024]{0,1:T(8,128)S(1)} fusion(f32[64,2048]{1,0:T(8,128)S(1)} %constant_dynamic-slice_fusion.5, f32[1024,64]{1,0:T(8,128)S(1)} %bitcast_select_fusion.5), kind=kOutput, calls=%fused_computation.78.clone.1 | convolution fusion | flops 1610612736 | bytes 9175040 | tf_op jit(solution)/shard_map/while/body/eval_jaxpr/dot_general | solution.py:51
  131.9 1.4 multiply_reduce_fusion.5
  134.6 6.7 %fusion.56 = f32[2048,1024]{0,1:T(8,128)S(1)} fusion(f32[64,2048]{1,0:T(8,128)S(1)} %constant_dynamic-slice_fusion.5, f32[1024,64]{1,0:T(8,128)S(1)} %bitcast_select_fusion.5), kind=kOutput, calls=%fused_computation.78.clone.1 | convolution fusion | flops 1610612736 | bytes 9175040 | tf_op jit(solution)/shard_map/while/body/eval_jaxpr/dot_general | solution.py:51
  141.3 1.4 multiply_reduce_fusion.5
  144.0 6.7 %fusion.56 = f32[2048,1024]{0,1:T(8,128)S(1)} fusion(f32[64,2048]{1,0:T(8,128)S(1)} %constant_dynamic-slice_fusion.5, f32[1024,64]{1,0:T(8,128)S(1)} %bitcast_select_fusion.5), kind=kOutput, calls=%fused_computation.78.clone.1 | convolution fusion | flops 1610612736 | bytes 9175040 | tf_op jit(solution)/shard_map/while/body/eval_jaxpr/dot_general | solution.py:51
  150.7 1.4 multiply_reduce_fusion.5
  152.1 2.8 %fusion.5 = f32[16,8192]{1,0:T(8,128)S(1)} fusion(f32[16,8192]{1,0:T(8,128)S(1)} %copy-done.2, f32[64,8192]{1,0:T(8,128)} %get-tuple-element.370, f32[16,8192]{1,0:T(8,128)S(1)} %get-tuple-element.164, f32[64,64]{1,0:T(8,128)S(1)} %convert_element_type.14, s32[]{:T(128)S(6)} %select_n.32), kind=kOutput, calls=%fused_computation.15 | convolution fusion | flops 101057536 | bytes 3678212 | tf_op jit(solution)/shard_map/dot_general | solution.py:58
  155.0 1.2 fusion.4
  156.2 1.1 reshape.50
  (69 shorter events, 13.8 us)
Async XLA Ops:
  6.5 9.9 %copy-start.8 = (f32[16]{0:T(128)S(1)}, f32[16]{0:T(128)}, u32[]{:S(2)}) copy-start(f32[16]{0:T(128)} %param.15) | copy-start | bytes 196
  6.5 42.4 %all-gather.3.cloned.1.call-start = ((), (), s32[]{:S(2)}) async-start(), calls=%async_computation | async-start | bytes 2621440 | tf_op jit(solution)/shard_map/all_gather | solution.py:107
  10.1 8.1 %collective-permute-start = (f32[19,4,1,512]{3,2,1,0:T(1,128)S(1)}, f32[19,4,1,512]{3,2,1,0:T(1,128)S(1)}, u32[]{:S(2)}, u32[]{:S(2)}) collective-permute-start(f32[19,4,1,512]{3,2,1,0:T(1,128)S(1)} %get-tuple-element.227), channel_id=1, source_target_pairs={{0,4},{4,8},{8,12},{12,16},{16,20},{20,24},{24,28},{1,5},{5,9},{9,... | collective-permute-start | bytes 466952 | tf_op jit(solution)/shard_map/ppermute | solution.py:15
  15.0 7.4 %collective-permute-start.1 = (f32[19,4,1,512]{3,2,1,0:T(1,128)S(1)}, f32[19,4,1,512]{3,2,1,0:T(1,128)S(1)}, u32[]{:S(2)}, u32[]{:S(2)}) collective-permute-start(f32[19,4,1,512]{3,2,1,0:T(1,128)S(1)} %get-tuple-element.228), channel_id=1, source_target_pairs={{4,0},{8,4},{12,8},{16,12},{20,16},{24,20},{28,24},{5,1},{9,5},{13... | collective-permute-start | bytes 466952 | tf_op jit(solution)/shard_map/ppermute | solution.py:15
  22.9 2.2 %copy-start.5 = (s32[64,64]{1,0:T(8,128)S(1)}, s32[64,64]{1,0:T(8,128)}, u32[]{:S(2)}) copy-start(s32[64,64]{1,0:T(8,128)} %param.17) | copy-start | bytes 49156
  22.9 2.2 %copy-start.7 = (f32[64]{0:T(128)S(1)}, f32[64]{0:T(128)}, u32[]{:S(2)}) copy-start(f32[64]{0:T(128)} %param.16) | copy-start | bytes 772
  22.9 2.3 %copy-start.6 = (s32[64,64]{1,0:T(8,128)S(1)}, s32[64,64]{1,0:T(8,128)}, u32[]{:S(2)}) copy-start(s32[64,64]{1,0:T(8,128)} %param.19) | copy-start | bytes 49156
  22.9 26.0 %copy-start.4 = (s32[64,64]{1,0:T(8,128)S(1)}, s32[64,64]{1,0:T(8,128)}, u32[]{:S(2)}) copy-start(s32[64,64]{1,0:T(8,128)} %param.18) | copy-start | bytes 49156
  24.8 89.5 %all-gather.5.cloned.1.call-start = ((), (), s32[]{:S(2)}) async-start(), calls=%async_computation.1 | async-start | bytes 2621440 | tf_op jit(solution)/shard_map/all_gather | solution.py:107
  49.0 37.6 %copy-start.3 = (f32[16,8192]{1,0:T(8,128)S(1)}, f32[16,8192]{1,0:T(8,128)}, u32[]{:S(2)}) copy-start(f32[16,8192]{1,0:T(8,128)} %reshape.49) | copy-start | bytes 1572868
  86.6 2.9 %copy-start = (f32[64,8192]{1,0:T(8,128)S(1)}, f32[64,8192]{1,0:T(8,128)}, u32[]{:S(2)}) copy-start(f32[64,8192]{1,0:T(8,128)} %get-tuple-element.368) | copy-start | bytes 6291460
  114.3 37.8 %copy-start.2 = (f32[16,8192]{1,0:T(8,128)S(1)}, f32[16,8192]{1,0:T(8,128)}, u32[]{:S(2)}) copy-start(f32[16,8192]{1,0:T(8,128)} %fusion.6) | copy-start | bytes 1572868
  152.1 2.9 %copy-start.1 = (f32[64,8192]{1,0:T(8,128)S(1)}, f32[64,8192]{1,0:T(8,128)}, u32[]{:S(2)}) copy-start(f32[64,8192]{1,0:T(8,128)} %get-tuple-element.370) | copy-start | bytes 6291460
Sparse Core Ops, SparseCore 0:
  24.9 23.9 all-gather.2
  91.7 22.5 all-gather.4
where the time goes:
time: 165 us; the launch traced here: 164 us
  matrix products  62.4 us (38%)
  waiting for transfers between devices  51.7 us (31%)
  other arithmetic  15.3 us (9%)
  local copies, waits for them, and re-layouts  14.1 us (9%)
  between operations  13.7 us (8%)
  starting transfers between devices  6.4 us (4%)
    dot_general x8, matrix products, add_block(): jnp.dot(pairs, cols, precision=lax.Precision.HIGHEST, preferred_element_t...  53.4 us
    all_gather x2, waiting for transfers between devices, body(): whole = lax.all_gather(current, 'cls', axis=0, tiled=True)  46.4 us
    reduce_sum x8, other arithmetic, add_block(): jnp.sum(made.reshape(total, count, block) * cols[:, None, :], axis=0)  10.9 us
    dynamic_slice x8, local copies, waits for them, and re-layouts, add_block(): cols = lax.dynamic_slice_in_dim(whole, offset, block, 1)  8.71 us
    ppermute x2, starting transfers between devices, passed_along(): return lax.ppermute(x, axis, pairs)  6.17 us
    dot_general x2, matrix products, react(): jnp.dot(kernel_rows, whole, precision=lax.Precision.HIGHEST, preferred_el...  5.69 us
    ppermute x2, waiting for transfers between devices, passed_along(): return lax.ppermute(x, axis, pairs)  5.32 us
  transfers between devices with their start and end apart: 4, of which 4 were waited for; matrix products, arithmetic and copies ran while one was open for 1% of the time, Pallas kernels for 0%

commit v1 on v0

--- a/solution.py
+++ b/solution.py
@@ -1,3 +1,4 @@
+import functools
 import jax
 import jax.numpy as jnp
 from jax import lax
@@ -7,6 +8,25 @@
 CX = 4
 kernel_scale = 1e-05
 temp_floats = 2097152
+
+
+def unite_sheet(obj, on_dim):
+    row_list = [obj]
+    n_peers_all = lax.axis_size("cls")
+    for k0 in tuple(range(n_peers_all - 1)):
+        row_list.append(
+            lax.ppermute(
+                row_list[-1], "cls", [(jj, (jj + 1) % n_peers_all) for jj in range(n_peers_all)]
+            )
+        )
+    return jnp.roll(
+        jnp.concatenate(row_list[::-1], on_dim),
+        (lax.axis_index("cls") + 1) * obj.shape[on_dim],
+        on_dim,
+    )
+
+
+attach_pairs_all = functools.partial(unite_sheet, on_dim=0)
 
 
 def passed_along(x, axis, by):
@@ -104,7 +124,7 @@
     start = lax.axis_index("cls") * group
     tables = make_tables(start, group, kernel_levels, pair_target, fragment_weights, breakage_rate)
     for sub in range(2):
-        whole = lax.all_gather(current, "cls", axis=0, tiled=True)
+        whole = attach_pairs_all(current)
         current = react(current, whole, tables, breakage_rate)
     return current.reshape(group, layers, columns)
 

time: 165 us -> 148 us (0.90)
  between operations: 13.7 us -> 0.26 us
  local copies, waits for them, and re-layouts: 14.1 us -> 6.25 us
  other arithmetic: 15.3 us -> 20.8 us
  matrix products: 62.4 us -> 58.1 us
  waiting for transfers between devices: 51.7 us -> 55.5 us
    ppermute x0 -> x6, waiting for transfers between devices: none -> 50.2 us  [unite_sheet(): lax.ppermute(row_list[-1], 'cls', [(jj, (jj + 1) % n_peers_all) for jj in...]
    all_gather x2 -> x0, waiting for transfers between devices: 46.4 us -> none  [body(): whole = lax.all_gather(current, 'cls', axis=0, tiled=True)]
    dynamic_slice x8, local copies, waits for them, and re-layouts: 8.71 us -> 0.34 us  [add_block(): cols = lax.dynamic_slice_in_dim(whole, offset, block, 1)]
    concatenate x0 -> x2, other arithmetic: none -> 5.51 us  [unite_sheet(): jnp.roll(jnp.concatenate(row_list[::-1], on_dim), (lax.axis_index('cls')...]
    dot_general x2, matrix products: 5.69 us -> 2.21 us  [react(): jnp.dot(kernel_rows, whole, precision=lax.Precision.HIGHEST, preferred_el...]
  transfers between devices with their start and end apart: 4 -> 8, of which waited for: 4 -> 8; matrix products, arithmetic and copies ran while one was open for 1% -> 1% of each run, Pallas kernels for 0% -> 0%
where the time goes in v1:
time: 148 us
  matrix products  58.1 us (39%)
  waiting for transfers between devices  55.5 us (38%)
  other arithmetic  20.8 us (14%)
  starting transfers between devices  6.3 us (4%)
  local copies, waits for them, and re-layouts  6.25 us (4%)
    dot_general x8, matrix products, add_block(): jnp.dot(pairs, cols, precision=lax.Precision.HIGHEST, preferred_element_t...  53.4 us
    ppermute x6, waiting for transfers between devices, unite_sheet(): lax.ppermute(row_list[-1], 'cls', [(jj, (jj + 1) % n_peers_all) for jj in...  50.2 us
    reduce_sum x8, other arithmetic, add_block(): jnp.sum(made.reshape(total, count, block) * cols[:, None, :], axis=0)  10.9 us
    ppermute x2, starting transfers between devices, passed_along(): return lax.ppermute(x, axis, pairs)  6.17 us
    concatenate x2, other arithmetic, unite_sheet(): jnp.roll(jnp.concatenate(row_list[::-1], on_dim), (lax.axis_index('cls')...  5.51 us
    ppermute x2, waiting for transfers between devices, passed_along(): return lax.ppermute(x, axis, pairs)  5.32 us
  transfers between devices with their start and end apart: 8, of which 8 were waited for; matrix products, arithmetic and copies ran while one was open for 1% of the time, Pallas kernels for 0%

profile of v1, /device:TPU:0, one launch (start us, length us, event | category | flops | bytes accessed | tf_op | source)
XLA Modules:
  0.0 148.0 jit_solution(4927708181805444738)
XLA Ops:
  0.0 1.5 %reshape.47 = f32[16,4,4,512]{3,2,1,0:T(4,128)S(1)} reshape(f32[16,4,2048]{2,1,0:T(4,128)} %param.14) | data formatting | bytes 1048576 | tf_op jit(solution)/shard_map/reshape | solution.py:104
  3.5 4.9 %collective-permute-start = (f32[19,4,1,512]{3,2,1,0:T(1,128)S(1)}, f32[19,4,1,512]{3,2,1,0:T(1,128)S(1)}, u32[]{:S(2)}, u32[]{:S(2)}) collective-permute-start(f32[19,4,1,512]{3,2,1,0:T(1,128)S(1)} %get-tuple-element.228), channel_id=1, source_target_pairs={{0,4},{4,8},{8,12},{12,16},{16,20},{20,24},{24,28},{1,5},{5,9},{9,... | collective-permute-start | bytes 466952 | tf_op jit(solution)/shard_map/ppermute | solution.py:35
  8.4 1.3 collective-permute-start.1
  11.7 4.1 %collective-permute-done.1 = f32[19,4,1,512]{3,2,1,0:T(1,128)S(1)} collective-permute-done((f32[19,4,1,512]{3,2,1,0:T(1,128)S(1)}, f32[19,4,1,512]{3,2,1,0:T(1,128)S(1)}, u32[]{:S(2)}, u32[]{:S(2)}) %collective-permute-start.1) | collective-permute-done | bytes 155680 | tf_op jit(solution)/shard_map/ppermute | solution.py:35
  17.4 8.6 %collective-permute-done.2 = f32[16,8192]{1,0:T(8,128)S(1)} collective-permute-done((f32[16,8192]{1,0:T(8,128)S(1)}, f32[16,8192]{1,0:T(8,128)S(1)}, u32[]{:S(2)}, u32[]{:S(2)}) %collective-permute-start.2) | collective-permute-done | bytes 524320 | tf_op jit(solution)/shard_map/ppermute | solution.py:18
  26.0 8.6 %collective-permute-done.3 = f32[16,8192]{1,0:T(8,128)S(1)} collective-permute-done((f32[16,8192]{1,0:T(8,128)S(1)}, f32[16,8192]{1,0:T(8,128)S(1)}, u32[]{:S(2)}, u32[]{:S(2)}) %collective-permute-start.3) | collective-permute-done | bytes 524320 | tf_op jit(solution)/shard_map/ppermute | solution.py:18
  35.4 7.9 %collective-permute-done.4 = f32[16,8192]{1,0:T(8,128)} collective-permute-done((f32[16,8192]{1,0:T(8,128)S(1)}, f32[16,8192]{1,0:T(8,128)}, u32[]{:S(2)}, u32[]{:S(2)}) %collective-permute-start.4) | collective-permute-done | bytes 524320 | tf_op jit(solution)/shard_map/ppermute | solution.py:18
  43.4 2.8 %fusion.18 = f32[64,8192]{1,0:T(8,128)S(1)} fusion(s32[]{:T(128)S(6)} %select_n.57, f32[16,8192]{1,0:T(8,128)} %collective-permute-done.4, f32[16,8192]{1,0:T(8,128)} %copy-done.1, f32[16,8192]{1,0:T(8,128)S(1)} %collective-permute-done.2, f32[16,8192]{1,0:T(8,128)S(1)} %reshape.49), kind=kLoop, calls=%fused_computation.46 | loop fusion | flops 3670016 | bytes 4194308 | tf_op jit(solution)/shard_map/jit(_roll_dynamic)/concatenate | solution.py:22
  46.2 33.6 %while.28 = (s32[]{:T(128)}, f32[16,8192]{1,0:T(8,128)S(1)}, f32[64,8192]{1,0:T(8,128)S(1)}, s32[64,64]{1,0:T(8,128)S(1)}, s32[1024]{0:T(1024)S(1)}, /*index=5*/...) while((s32[]{:T(128)}, f32[16,8192]{1,0:T(8,128)S(1)}, ...), condition=%wide.region_2.4_spmd.clone, body=%wide.region_0.3_spmd.clone.sunk | while | flops 1614905344 | bytes 19828892 | solution.py:77
  46.6 6.7 %fusion.65 = f32[2048,1024]{0,1:T(8,128)S(1)} fusion(f32[64,2048]{1,0:T(8,128)S(1)} %constant_dynamic-slice_fusion.4, f32[1024,64]{1,0:T(8,128)S(1)} %bitcast_select_fusion.4), kind=kOutput, calls=%fused_computation.105.clone.1 | convolution fusion | flops 1610612736 | bytes 9175040 | tf_op jit(solution)/shard_map/while/body/eval_jaxpr/dot_general | solution.py:71
  53.3 1.4 multiply_reduce_fusion.4
  55.0 6.7 %fusion.65 = f32[2048,1024]{0,1:T(8,128)S(1)} fusion(f32[64,2048]{1,0:T(8,128)S(1)} %constant_dynamic-slice_fusion.4, f32[1024,64]{1,0:T(8,128)S(1)} %bitcast_select_fusion.4), kind=kOutput, calls=%fused_computation.105.clone.1 | convolution fusion | flops 1610612736 | bytes 9175040 | tf_op jit(solution)/shard_map/while/body/eval_jaxpr/dot_general | solution.py:71
  61.7 1.4 multiply_reduce_fusion.4
  63.3 6.7 %fusion.65 = f32[2048,1024]{0,1:T(8,128)S(1)} fusion(f32[64,2048]{1,0:T(8,128)S(1)} %constant_dynamic-slice_fusion.4, f32[1024,64]{1,0:T(8,128)S(1)} %bitcast_select_fusion.4), kind=kOutput, calls=%fused_computation.105.clone.1 | convolution fusion | flops 1610612736 | bytes 9175040 | tf_op jit(solution)/shard_map/while/body/eval_jaxpr/dot_general | solution.py:71
  70.0 1.4 multiply_reduce_fusion.4
  71.7 6.7 %fusion.65 = f32[2048,1024]{0,1:T(8,128)S(1)} fusion(f32[64,2048]{1,0:T(8,128)S(1)} %constant_dynamic-slice_fusion.4, f32[1024,64]{1,0:T(8,128)S(1)} %bitcast_select_fusion.4), kind=kOutput, calls=%fused_computation.105.clone.1 | convolution fusion | flops 1610612736 | bytes 9175040 | tf_op jit(solution)/shard_map/while/body/eval_jaxpr/dot_general | solution.py:71
  78.4 1.4 multiply_reduce_fusion.4
  80.9 1.2 fusion.6
  82.2 8.6 %collective-permute-done.5 = f32[16,8192]{1,0:T(8,128)S(1)} collective-permute-done((f32[16,8192]{1,0:T(8,128)S(1)}, f32[16,8192]{1,0:T(8,128)S(1)}, u32[]{:S(2)}, u32[]{:S(2)}) %collective-permute-start.5) | collective-permute-done | bytes 524320 | tf_op jit(solution)/shard_map/ppermute | solution.py:18
  90.8 8.6 %collective-permute-done.6 = f32[16,8192]{1,0:T(8,128)S(1)} collective-permute-done((f32[16,8192]{1,0:T(8,128)S(1)}, f32[16,8192]{1,0:T(8,128)S(1)}, u32[]{:S(2)}, u32[]{:S(2)}) %collective-permute-start.6) | collective-permute-done | bytes 524320 | tf_op jit(solution)/shard_map/ppermute | solution.py:18
  100.2 7.9 %collective-permute-done.7 = f32[16,8192]{1,0:T(8,128)} collective-permute-done((f32[16,8192]{1,0:T(8,128)S(1)}, f32[16,8192]{1,0:T(8,128)}, u32[]{:S(2)}, u32[]{:S(2)}) %collective-permute-start.7) | collective-permute-done | bytes 524320 | tf_op jit(solution)/shard_map/ppermute | solution.py:18
  108.1 2.8 %fusion.11 = f32[64,8192]{1,0:T(8,128)S(1)} fusion(s32[]{:T(128)S(6)} %select_n.57, f32[16,8192]{1,0:T(8,128)} %collective-permute-done.7, f32[16,8192]{1,0:T(8,128)} %copy-done.2, f32[16,8192]{1,0:T(8,128)S(1)} %collective-permute-done.5, f32[16,8192]{1,0:T(8,128)S(1)} %fusion.6), kind=kLoop, calls=%fused_computation.39 | loop fusion | flops 3670016 | bytes 4194308 | tf_op jit(solution)/shard_map/jit(_roll_dynamic)/concatenate | solution.py:22
  110.9 33.6 %while.29 = (s32[]{:T(128)}, f32[16,8192]{1,0:T(8,128)S(1)}, f32[64,8192]{1,0:T(8,128)S(1)}, s32[64,64]{1,0:T(8,128)S(1)}, s32[1024]{0:T(1024)S(1)}, /*index=5*/...) while((s32[]{:T(128)}, f32[16,8192]{1,0:T(8,128)S(1)}, ...), condition=%wide.region_6.8_spmd.clone, body=%wide.region_4.7_spmd.clone.sunk | while | flops 1614905344 | bytes 19828892 | solution.py:77
  111.4 6.7 %fusion.68 = f32[2048,1024]{0,1:T(8,128)S(1)} fusion(f32[64,2048]{1,0:T(8,128)S(1)} %constant_dynamic-slice_fusion.5, f32[1024,64]{1,0:T(8,128)S(1)} %bitcast_select_fusion.5), kind=kOutput, calls=%fused_computation.106.clone.1 | convolution fusion | flops 1610612736 | bytes 9175040 | tf_op jit(solution)/shard_map/while/body/eval_jaxpr/dot_general | solution.py:71
  118.1 1.4 multiply_reduce_fusion.5
  119.8 6.7 %fusion.68 = f32[2048,1024]{0,1:T(8,128)S(1)} fusion(f32[64,2048]{1,0:T(8,128)S(1)} %constant_dynamic-slice_fusion.5, f32[1024,64]{1,0:T(8,128)S(1)} %bitcast_select_fusion.5), kind=kOutput, calls=%fused_computation.106.clone.1 | convolution fusion | flops 1610612736 | bytes 9175040 | tf_op jit(solution)/shard_map/while/body/eval_jaxpr/dot_general | solution.py:71
  126.4 1.4 multiply_reduce_fusion.5
  128.1 6.7 %fusion.68 = f32[2048,1024]{0,1:T(8,128)S(1)} fusion(f32[64,2048]{1,0:T(8,128)S(1)} %constant_dynamic-slice_fusion.5, f32[1024,64]{1,0:T(8,128)S(1)} %bitcast_select_fusion.5), kind=kOutput, calls=%fused_computation.106.clone.1 | convolution fusion | flops 1610612736 | bytes 9175040 | tf_op jit(solution)/shard_map/while/body/eval_jaxpr/dot_general | solution.py:71
  134.8 1.4 multiply_reduce_fusion.5
  136.5 6.7 %fusion.68 = f32[2048,1024]{0,1:T(8,128)S(1)} fusion(f32[64,2048]{1,0:T(8,128)S(1)} %constant_dynamic-slice_fusion.5, f32[1024,64]{1,0:T(8,128)S(1)} %bitcast_select_fusion.5), kind=kOutput, calls=%fused_computation.106.clone.1 | convolution fusion | flops 1610612736 | bytes 9175040 | tf_op jit(solution)/shard_map/while/body/eval_jaxpr/dot_general | solution.py:71
  143.1 1.4 multiply_reduce_fusion.5
  145.7 1.2 fusion.4
  (73 shorter events, 12.6 us)
Async XLA Ops:
  0.0 9.9 %copy-start.6 = (f32[16]{0:T(128)S(1)}, f32[16]{0:T(128)}, u32[]{:S(2)}) copy-start(f32[16]{0:T(128)} %param.17) | copy-start | bytes 196
  3.5 8.1 %collective-permute-start = (f32[19,4,1,512]{3,2,1,0:T(1,128)S(1)}, f32[19,4,1,512]{3,2,1,0:T(1,128)S(1)}, u32[]{:S(2)}, u32[]{:S(2)}) collective-permute-start(f32[19,4,1,512]{3,2,1,0:T(1,128)S(1)} %get-tuple-element.228), channel_id=1, source_target_pairs={{0,4},{4,8},{8,12},{12,16},{16,20},{20,24},{24,28},{1,5},{5,9},{9,... | collective-permute-start | bytes 466952 | tf_op jit(solution)/shard_map/ppermute | solution.py:35
  8.4 7.4 %collective-permute-start.1 = (f32[19,4,1,512]{3,2,1,0:T(1,128)S(1)}, f32[19,4,1,512]{3,2,1,0:T(1,128)S(1)}, u32[]{:S(2)}, u32[]{:S(2)}) collective-permute-start(f32[19,4,1,512]{3,2,1,0:T(1,128)S(1)} %get-tuple-element.229), channel_id=1, source_target_pairs={{4,0},{8,4},{12,8},{16,12},{20,16},{24,20},{28,24},{5,1},{9,5},{13... | collective-permute-start | bytes 466952 | tf_op jit(solution)/shard_map/ppermute | solution.py:35
  16.3 18.4 %copy-start.3 = (s32[64,64]{1,0:T(8,128)S(1)}, s32[64,64]{1,0:T(8,128)}, u32[]{:S(2)}) copy-start(s32[64,64]{1,0:T(8,128)} %param.19) | copy-start | bytes 49156
  16.3 18.4 %copy-start.5 = (f32[64]{0:T(128)S(1)}, f32[64]{0:T(128)}, u32[]{:S(2)}) copy-start(f32[64]{0:T(128)} %param.18) | copy-start | bytes 772
  16.4 18.5 %copy-start.4 = (s32[64,64]{1,0:T(8,128)S(1)}, s32[64,64]{1,0:T(8,128)}, u32[]{:S(2)}) copy-start(s32[64,64]{1,0:T(8,128)} %param.21) | copy-start | bytes 49156
  17.4 8.7 %collective-permute-start.2 = (f32[16,8192]{1,0:T(8,128)S(1)}, f32[16,8192]{1,0:T(8,128)S(1)}, u32[]{:S(2)}, u32[]{:S(2)}) collective-permute-start(f32[16,8192]{1,0:T(8,128)S(1)} %reshape.49), channel_id=1, source_target_pairs={{0,1},{1,2},{2,3},{3,0},{4,5},{5,6},{6,7},{7,4},{8,9},{9,10},{10,1... | collective-permute-start | bytes 1572872 | tf_op jit(solution)/shard_map/ppermute | solution.py:18
  26.0 8.6 %collective-permute-start.3 = (f32[16,8192]{1,0:T(8,128)S(1)}, f32[16,8192]{1,0:T(8,128)S(1)}, u32[]{:S(2)}, u32[]{:S(2)}) collective-permute-start(f32[16,8192]{1,0:T(8,128)S(1)} %collective-permute-done.2), channel_id=1, source_target_pairs={{0,1},{1,2},{2,3},{3,0},{4,5},{5,6},{6,7},{7,4},{8,9},{9,10},{10,1... | collective-permute-start | bytes 1572872 | tf_op jit(solution)/shard_map/ppermute | solution.py:18
  34.6 0.8 copy-start.1
  34.6 8.7 %collective-permute-start.4 = (f32[16,8192]{1,0:T(8,128)S(1)}, f32[16,8192]{1,0:T(8,128)}, u32[]{:S(2)}, u32[]{:S(2)}) collective-permute-start(f32[16,8192]{1,0:T(8,128)S(1)} %collective-permute-done.3), channel_id=1, source_target_pairs={{0,1},{1,2},{2,3},{3,0},{4,5},{5,6},{6,7},{7,4},{8,9},{9,10},{10,1... | collective-permute-start | bytes 1572872 | tf_op jit(solution)/shard_map/ppermute | solution.py:18
  35.4 10.7 %copy-start = (s32[64,64]{1,0:T(8,128)S(1)}, s32[64,64]{1,0:T(8,128)}, u32[]{:S(2)}) copy-start(s32[64,64]{1,0:T(8,128)} %param.20) | copy-start | bytes 49156
  82.1 8.7 %collective-permute-start.5 = (f32[16,8192]{1,0:T(8,128)S(1)}, f32[16,8192]{1,0:T(8,128)S(1)}, u32[]{:S(2)}, u32[]{:S(2)}) collective-permute-start(f32[16,8192]{1,0:T(8,128)S(1)} %fusion.6), channel_id=1, source_target_pairs={{0,1},{1,2},{2,3},{3,0},{4,5},{5,6},{6,7},{7,4},{8,9},{9,10},{10,1... | collective-permute-start | bytes 1572872 | tf_op jit(solution)/shard_map/ppermute | solution.py:18
  90.8 8.6 %collective-permute-start.6 = (f32[16,8192]{1,0:T(8,128)S(1)}, f32[16,8192]{1,0:T(8,128)S(1)}, u32[]{:S(2)}, u32[]{:S(2)}) collective-permute-start(f32[16,8192]{1,0:T(8,128)S(1)} %collective-permute-done.5), channel_id=1, source_target_pairs={{0,1},{1,2},{2,3},{3,0},{4,5},{5,6},{6,7},{7,4},{8,9},{9,10},{10,1... | collective-permute-start | bytes 1572872 | tf_op jit(solution)/shard_map/ppermute | solution.py:18
  99.4 0.8 copy-start.2
  99.4 8.7 %collective-permute-start.7 = (f32[16,8192]{1,0:T(8,128)S(1)}, f32[16,8192]{1,0:T(8,128)}, u32[]{:S(2)}, u32[]{:S(2)}) collective-permute-start(f32[16,8192]{1,0:T(8,128)S(1)} %collective-permute-done.6), channel_id=1, source_target_pairs={{0,1},{1,2},{2,3},{3,0},{4,5},{5,6},{6,7},{7,4},{8,9},{9,10},{10,1... | collective-permute-start | bytes 1572872 | tf_op jit(solution)/shard_map/ppermute | solution.py:18
